TPU v7x, 32 devices: a whole 2x2x4 slice. The times are simulated.
32 devices in a mesh: layer: 4 (over y, x), row: 2 (over core), col: 4 (over z).
Axes of the slice: x: 2, y: 2, z: 4, core: 2. Of those that a mesh axis runs over, the one named last changes fastest.
Arguments:
- hidden: bfloat16 [384, 2304], P(('layer', 'row')), may hold values from -60 to 60
- embedding: bfloat16 [16384, 2304], P(('row', 'col'), 'layer'), may hold values from -0.3 to 0.3
- teacher: bfloat16 [384, 16384], P('layer', ('row', 'col')), may hold values from -80 to 240
Outputs:
- grad_embedding: float32 [16384, 2304], P(('row', 'col'), 'layer')
- grad_hidden: float32 [384, 2304], P(('layer', 'row', 'col'))
All inputs are finite; a program needn't handle non-finite values.
Results may differ from a plain program's by a relative error of at most 0.0041.
Values may be sent and summed in bfloat16 or wider, within the bound.
A program may use at most 192 MiB of HBM per device.

v0:
```python
import jax
import jax.numpy as jnp
from jax import lax
from jax.sharding import PartitionSpec as P

LOSS_SCALE = 256


def local(hidden, embedding, teacher):
    token_rows = lax.all_gather(hidden, "row", axis=0, tiled=True)
    width_part = lax.all_to_all(token_rows, "layer", split_axis=1, concat_axis=0, tiled=True)
    logits = lax.psum_scatter(
        lax.dot_general(
            width_part, embedding, (((1,), (1,)), ((), ())), preferred_element_type=jnp.float32
        ),
        "layer",
        scatter_dimension=0,
        tiled=True,
    )
    teach_f = teacher.astype(jnp.float32)
    top_s, top_t = lax.pmax((jnp.max(logits, axis=1), jnp.max(teach_f, axis=1)), ("row", "col"))
    part_s = jnp.sum(jnp.exp(logits - top_s[:, None]), axis=1)
    part_t = jnp.sum(jnp.exp(teach_f - top_t[:, None]), axis=1)
    sum_s, sum_t = lax.psum((part_s, part_t), ("row", "col"))
    lse_s = top_s + jnp.log(sum_s)
    lse_t = top_t + jnp.log(sum_t)
    prob_s = jnp.exp(logits - lse_s[:, None])
    prob_t = jnp.exp(teach_f - lse_t[:, None])
    grads = ((prob_s - prob_t) * LOSS_SCALE).astype(jnp.bfloat16)
    grad_piece = lax.all_gather(grads, "layer", axis=0, tiled=True)
    embed_acc = lax.dot_general(
        grad_piece, width_part, (((0,), (0,)), ((), ())), preferred_element_type=jnp.float32
    )
    hidden_piece = jnp.dot(grad_piece, embedding, preferred_element_type=jnp.float32)
    hidden_terms = lax.all_to_all(hidden_piece, "layer", split_axis=0, concat_axis=1, tiled=True)
    grad_hidden = lax.psum_scatter(hidden_terms, ("row", "col"), scatter_dimension=0, tiled=True)
    return (embed_acc, grad_hidden)


def solution(mesh):
    placed = (P(("layer", "row"), None), P(("row", "col"), "layer"), P("layer", ("row", "col")))
    return jax.shard_map(
        local,
        mesh=mesh,
        in_specs=placed,
        out_specs=(P(("row", "col"), "layer"), P(("layer", "row", "col"), None)),
        check_vma=False,
    )
```

profile of v0, /device:TPU:1, one launch (start us, length us, event | category | flops | bytes accessed | tf_op | source)
XLA Modules:
  0.0 216.0 jit_solution(10763876937868347929)
XLA Ops:
  7.2 0.0 copy-start
  7.2 0.0 reduce-scatter.4.cloned.1.call-start
  7.2 2.5 %all_gather.6 = bf16[96,2304]{1,0:T(8,128)(2,1)S(1)} all-gather(bf16[48,2304]{1,0:T(8,128)(2,1)} %param.3), channel_id=1, replica_groups=mesh['layer'=4,'row'=2,'col'=4] {'row'}, dimensions={0}, use_global_device_ids=true | all-gather | bytes 663552 | tf_op jit(solution)/shard_map/all_gather | solution.py:10
  9.7 0.6 all_to_all.28
  10.3 0.1 copy.11
  10.3 11.5 %all_to_all.38 = bf16[96,4,576]{2,0,1:T(8,128)(2,1)S(1)} all-to-all(bf16[96,4,576]{2,0,1:T(8,128)(2,1)S(1)} %copy.11), channel_id=1, replica_groups=mesh['layer'=4,'row'=2,'col'=4] {'layer'}, dimensions={1} | all-to-all | bytes 884736 | tf_op jit(solution)/shard_map/all_to_all | solution.py:11
  21.8 0.0 copy-start.2
  21.8 0.8 copy-done.2
  22.6 0.0 copy-done
  22.6 3.1 %fusion.7 = f32[384,2048]{1,0:T(8,128)} fusion(bf16[384,576]{1,0:T(8,128)(2,1)S(1)} %bitcast.14, bf16[2048,576]{0,1:T(8,128)(2,1)S(1)} %copy-done), kind=kOutput, calls=%fused_computation.12 | convolution fusion | flops 905969664 | bytes 5947392 | tf_op jit(solution)/shard_map/dot_general | solution.py:13
  25.7 0.0 copy-start.5
  25.7 0.0 reduce-scatter.4.cloned.1.call-update
  25.7 0.0 all-gather.2.cloned.1.call-start
  25.8 0.9 copy-done.5
  26.7 0.2 reduce_max.24
  26.8 43.8 %reduce-scatter.4.cloned.1.call-done = f32[96,2048]{1,0:T(8,128)} async-done(((f32[384,2048]{1,0:T(8,128)}), f32[96,2048]{1,0:T(8,128)}) %reduce-scatter.4.cloned.1.call-update) | async-done | bytes 786448 | tf_op jit(solution)/shard_map/reduce_scatter | solution.py:12
  70.6 0.0 copy-start.1
  70.6 1.3 reduce_max.23
  72.0 17.8 %all-reduce.3 = (f32[96]{0:T(128)S(1)}, f32[96]{0:T(128)S(1)}) all-reduce(bf16[96]{0:T(256)(128)(2,1)S(1)} %reduce_max.24, f32[96]{0:T(128)S(1)} %reduce_max.23), channel_id=1, replica_groups=mesh['layer'=4,'row'=2,'col'=4] {'row','col'}, use_global_device_ids=true, to_apply=%region_6.0 | all-reduce | flops 192 | bytes 1344 | tf_op jit(solution)/shard_map/pmax | solution.py:21
  89.8 1.5 fusion.2
  91.4 14.2 %all-reduce.2 = (f32[96]{0:T(128)}, f32[96]{0:T(128)}) all-reduce(f32[96]{0:T(128)S(1)} %get-tuple-element.6, f32[96]{0:T(128)S(1)} %get-tuple-element.7), channel_id=1, replica_groups=mesh['layer'=4,'row'=2,'col'=4] {'row','col'}, use_global_device_ids=true, to_apply=%region_8.0 | all-reduce | flops 192 | bytes 1536 | tf_op jit(solution)/shard_map/psum | solution.py:24
  105.6 0.7 log_add_fusion
  106.2 0.7 log_add_fusion.1
  106.9 0.0 copy-done.1
  106.9 1.1 fusion.6
  108.0 0.0 all-gather.2.cloned.1.call-update
  108.0 0.0 copy-start.6
  108.0 29.8 %all-gather.2.cloned.1.call-done = bf16[384,2048]{1,0:T(8,128)(2,1)} async-done(((bf16[96,2048]{1,0:T(8,128)(2,1)}), bf16[384,2048]{1,0:T(8,128)(2,1)}) %all-gather.2.cloned.1.call-update) | async-done | bytes 1572880 | tf_op jit(solution)/shard_map/all_gather | solution.py:30
  137.8 3.8 %fusion.9 = f32[384,576]{1,0:T(8,128)} fusion(bf16[384,2048]{1,0:T(8,128)(2,1)} %all-gather.2.cloned.1.call-done, bf16[2048,576]{0,1:T(8,128)(2,1)S(1)} %copy-done), kind=kOutput, calls=%fused_computation.14 | convolution fusion | flops 905969664 | bytes 4816896 | tf_op jit(solution)/shard_map/dot_general | solution.py:34
  141.6 3.5 %all-to-all-start.1 = ((f32[4,96,576]{2,1,0:T(8,128)}), f32[4,96,576]{2,1,0:T(8,128)S(1)}, u32[]{:S(2)}, u32[]{:S(2)}) async-start(f32[4,96,576]{2,1,0:T(8,128)} %bitcast.17), calls=%async_computation.2 | async-start | bytes 1966080 | tf_op jit(solution)/shard_map/all_to_all | solution.py:35
  145.1 0.0 copy-done.6
  145.1 0.6 dynamic-slice.4
  146.3 11.2 %all-to-all-done.1 = f32[4,96,576]{2,1,0:T(8,128)S(1)} async-done(((f32[4,96,576]{2,1,0:T(8,128)}), f32[4,96,576]{2,1,0:T(8,128)S(1)}, u32[]{:S(2)}, u32[]{:S(2)}) %all-to-all-start.1) | async-done | bytes 884768 | tf_op jit(solution)/shard_map/all_to_all | solution.py:35
  157.5 0.0 copy-start.4
  157.5 0.9 copy-done.4
  158.4 0.0 copy-start.3
  158.4 2.8 %copy.13 = f32[96,4,576]{2,1,0:T(4,128)} copy(f32[96,4,576]{2,0,1:T(8,128)} %bitcast.16) | data formatting | bytes 1769472 | tf_op jit(solution)/shard_map/all_to_all | solution.py:35
  161.3 2.7 %all_to_all.35 = f32[96,2304]{1,0:T(8,128)} reshape(f32[96,4,576]{2,1,0:T(4,128)} %copy.13) | data formatting | bytes 1769472 | tf_op jit(solution)/shard_map/all_to_all | solution.py:35
  164.0 32.7 %fusion = f32[16,2304]{1,0:T(8,128)S(1)} fusion(f32[96,2304]{1,0:T(8,128)} %all_to_all.35), kind=kCustom, calls=%all-reduce-scatter | all-reduce-scatter fusion | flops 294913 | bytes 1032704
  196.7 1.9 collective-permute-start
  198.6 2.4 %collective-permute-start.1 = (f32[12,2304]{1,0:T(8,128)S(1)}, f32[12,2304]{1,0:T(8,128)S(1)}, u32[]{:S(2)}, u32[]{:S(2)}) collective-permute-start(f32[12,2304]{1,0:T(8,128)S(1)} %slice), channel_id=1, source_target_pairs={{0,2},{1,3},{2,4},{3,5},{4,6},{5,7},{8,10},{9,11},{10,12},{11,13},... | collective-permute-start | bytes 331784
  201.0 0.0 copy-done.3
  201.0 5.0 %fusion.8 = f32[2048,576]{0,1:T(8,128)} fusion(bf16[384,2048]{1,0:T(8,128)(2,1)} %all-gather.2.cloned.1.call-done, bf16[384,576]{1,0:T(8,128)(2,1)S(1)} %bitcast.15), kind=kOutput, calls=%fused_computation.13 | convolution fusion | flops 905969664 | bytes 6733824 | tf_op jit(solution)/shard_map/dot_general | solution.py:31
  206.1 2.0 collective-permute-done.1
  208.1 0.0 collective-permute-done
  208.1 0.4 concatenate
  208.5 0.7 constant_dynamic-slice_fusion
  (1 shorter events, 0.0 us)
Async XLA Ops:
  7.2 15.5 %copy-start = (bf16[2048,576]{0,1:T(8,128)(2,1)S(1)}, bf16[2048,576]{0,1:T(8,128)(2,1)}, u32[]{:S(2)}) copy-start(bf16[2048,576]{0,1:T(8,128)(2,1)} %param.4) | copy-start | bytes 7077892
  7.2 63.5 %reduce-scatter.4.cloned.1.call-start = ((), (), s32[]{:S(2)}) async-start(), calls=%async_computation.3 | async-start | bytes 3932160 | tf_op jit(solution)/shard_map/reduce_scatter | solution.py:12
  21.8 0.8 copy-start.2
  25.7 1.0 copy-start.5
  25.7 112.1 %all-gather.2.cloned.1.call-start = ((), (), s32[]{:S(2)}) async-start(), calls=%async_computation.4 | async-start | bytes 1966080 | tf_op jit(solution)/shard_map/all_gather | solution.py:30
  70.6 36.2 %copy-start.1 = (f32[96,2048]{1,0:T(8,128)S(1)}, f32[96,2048]{1,0:T(8,128)}, u32[]{:S(2)}) copy-start(f32[96,2048]{1,0:T(8,128)} %reduce-scatter.4.cloned.1.call-done) | copy-start | bytes 2359300
  108.0 37.1 %copy-start.6 = (u32[32]{0:T(128)S(1)}, u32[32]{0:T(128)}, u32[]{:S(2)}) copy-start(u32[32]{0:T(128)} %constant.10) | copy-start | bytes 388
  141.6 15.9 %all-to-all-start.1 = ((f32[4,96,576]{2,1,0:T(8,128)}), f32[4,96,576]{2,1,0:T(8,128)S(1)}, u32[]{:S(2)}, u32[]{:S(2)}) async-start(f32[4,96,576]{2,1,0:T(8,128)} %bitcast.17), calls=%async_computation.2 | async-start | bytes 1966080 | tf_op jit(solution)/shard_map/all_to_all | solution.py:35
  157.5 0.9 copy-start.4
  158.4 42.6 %copy-start.3 = (bf16[96,4,576]{2,0,1:T(8,128)(2,1)S(1)}, bf16[96,4,576]{2,0,1:T(8,128)(2,1)}, u32[]{:S(2)}) copy-start(bf16[96,4,576]{2,0,1:T(8,128)(2,1)} %copy-done.2) | copy-start | bytes 1327108
  196.7 11.4 %collective-permute-start = (f32[16,2304]{1,0:T(8,128)S(1)}, f32[16,2304]{1,0:T(8,128)S(1)}, u32[]{:S(2)}, u32[]{:S(2)}) collective-permute-start(f32[16,2304]{1,0:T(8,128)S(1)} %fusion), channel_id=1, source_target_pairs={{0,1},{1,2},{2,3},{3,4},{4,5},{5,6},{6,7},{8,9},{9,10},{10,11},{11... | collective-permute-start | bytes 442376
  198.6 9.5 %collective-permute-start.1 = (f32[12,2304]{1,0:T(8,128)S(1)}, f32[12,2304]{1,0:T(8,128)S(1)}, u32[]{:S(2)}, u32[]{:S(2)}) collective-permute-start(f32[12,2304]{1,0:T(8,128)S(1)} %slice), channel_id=1, source_target_pairs={{0,2},{1,3},{2,4},{3,5},{4,6},{5,7},{8,10},{9,11},{10,12},{11,13},... | collective-permute-start | bytes 331784
Sparse Core Ops, SparseCore 0:
  25.8 44.7 reduce-scatter.3
  108.1 29.6 all-gather.1
where the time goes:
time: 217 us; the launch traced here: 216 us
  waiting for transfers between devices  86.8 us (40%)
  blocking collectives  78.7 us (36%)
  between operations  14.8 us (7%)
  matrix products  11.9 us (5%)
  local copies, waits for them, and re-layouts  10.5 us (5%)
  starting transfers between devices  7.91 us (4%)
  other arithmetic  5.41 us (2%)
    reduce_scatter x1, waiting for transfers between devices, local(): lax.psum_scatter(lax.dot_general(width_part, embedding, (((1,), (1,)), ((...  43.8 us
    unnamed x1, blocking collectives  32.7 us
    all_gather x1, waiting for transfers between devices, local(): grad_piece = lax.all_gather(grads, 'layer', axis=0, tiled=True)  29.8 us
    pmax x1, blocking collectives, local(): lax.pmax((jnp.max(logits, axis=1), jnp.max(teach_f, axis=1)), ('row', 'co...  17.8 us
    psum x1, blocking collectives, local(): sum_s, sum_t = lax.psum((part_s, part_t), ('row', 'col'))  14.2 us
    all_to_all x1, blocking collectives, local(): lax.all_to_all(token_rows, 'layer', split_axis=1, concat_axis=0, tiled=True)  11.5 us
    all_to_all x1, waiting for transfers between devices, local(): lax.all_to_all(hidden_piece, 'layer', split_axis=0, concat_axis=1, tiled=...  11.2 us
    all_to_all x2, local copies, waits for them, and re-layouts, local(): lax.all_to_all(hidden_piece, 'layer', split_axis=0, concat_axis=1, tiled=...  5.53 us
  transfers between devices with their start and end apart: 5, of which 4 were waited for; matrix products, arithmetic and copies ran while one was open for 3% of the time, Pallas kernels for 0%

commit v1 on v0

--- a/solution.py
+++ b/solution.py
@@ -4,6 +4,11 @@
 from jax.sharding import PartitionSpec as P
 
 LOSS_SCALE = 256
+
+
+def axis_by_axis(array, inner_axis, outer_axis):
+    partial = lax.psum(array, inner_axis)
+    return lax.psum(partial, outer_axis)
 
 
 def local(hidden, embedding, teacher):
@@ -21,7 +26,7 @@
     top_s, top_t = lax.pmax((jnp.max(logits, axis=1), jnp.max(teach_f, axis=1)), ("row", "col"))
     part_s = jnp.sum(jnp.exp(logits - top_s[:, None]), axis=1)
     part_t = jnp.sum(jnp.exp(teach_f - top_t[:, None]), axis=1)
-    sum_s, sum_t = lax.psum((part_s, part_t), ("row", "col"))
+    sum_s, sum_t = axis_by_axis((part_s, part_t), "row", "col")
     lse_s = top_s + jnp.log(sum_s)
     lse_t = top_t + jnp.log(sum_t)
     prob_s = jnp.exp(logits - lse_s[:, None])

time: 217 us -> 212 us (0.977)
  blocking collectives: 78.7 us -> 74.2 us
    psum x1 -> x2, blocking collectives: 14.2 us -> 9.72 us  [the longest x1 6.73 us: axis_by_axis(): return lax.psum(partial, outer_axis)]
where the time goes in v1:
time: 212 us; the launch traced here: 211 us
  waiting for transfers between devices  87.8 us (41%)
  blocking collectives  74.2 us (35%)
  between operations  14.8 us (7%)
  matrix products  11.9 us (6%)
  local copies, waits for them, and re-layouts  10.5 us (5%)
  starting transfers between devices  7.91 us (4%)
  other arithmetic  4.11 us (2%)
    reduce_scatter x1, waiting for transfers between devices, local(): lax.psum_scatter(lax.dot_general(width_part, embedding, (((1,), (1,)), ((...  43.8 us
    unnamed x1, blocking collectives  32.7 us
    all_gather x1, waiting for transfers between devices, local(): grad_piece = lax.all_gather(grads, 'layer', axis=0, tiled=True)  30.7 us
    pmax x1, blocking collectives, local(): lax.pmax((jnp.max(logits, axis=1), jnp.max(teach_f, axis=1)), ('row', 'co...  17.8 us
    all_to_all x1, blocking collectives, local(): lax.all_to_all(token_rows, 'layer', split_axis=1, concat_axis=0, tiled=True)  11.5 us
    all_to_all x1, waiting for transfers between devices, local(): lax.all_to_all(hidden_piece, 'layer', split_axis=0, concat_axis=1, tiled=...  11.2 us
    psum x1, blocking collectives, axis_by_axis(): return lax.psum(partial, outer_axis)  6.73 us
    all_to_all x2, local copies, waits for them, and re-layouts, local(): lax.all_to_all(hidden_piece, 'layer', split_axis=0, concat_axis=1, tiled=...  5.53 us
  transfers between devices with their start and end apart: 5, of which 4 were waited for; matrix products, arithmetic and copies ran while one was open for 3% of the time, Pallas kernels for 0%

profile of v1, /device:TPU:1, one launch (start us, length us, event | category | flops | bytes accessed | tf_op | source)
XLA Modules:
  0.0 211.2 jit_solution(16825803821972433941)
XLA Ops:
  7.2 0.0 copy-start
  7.2 0.0 reduce-scatter.4.cloned.1.call-start
  7.2 2.5 %all_gather.6 = bf16[96,2304]{1,0:T(8,128)(2,1)S(1)} all-gather(bf16[48,2304]{1,0:T(8,128)(2,1)} %param.3), channel_id=1, replica_groups=mesh['layer'=4,'row'=2,'col'=4] {'row'}, dimensions={0}, use_global_device_ids=true | all-gather | bytes 663552 | tf_op jit(solution)/shard_map/all_gather | solution.py:15
  9.7 0.6 all_to_all.28
  10.3 0.1 copy.11
  10.3 11.5 %all_to_all.38 = bf16[96,4,576]{2,0,1:T(8,128)(2,1)S(1)} all-to-all(bf16[96,4,576]{2,0,1:T(8,128)(2,1)S(1)} %copy.11), channel_id=1, replica_groups=mesh['layer'=4,'row'=2,'col'=4] {'layer'}, dimensions={1} | all-to-all | bytes 884736 | tf_op jit(solution)/shard_map/all_to_all | solution.py:16
  21.8 0.0 copy-start.2
  21.8 0.8 copy-done.2
  22.6 0.0 copy-done
  22.6 3.1 %fusion.7 = f32[384,2048]{1,0:T(8,128)} fusion(bf16[384,576]{1,0:T(8,128)(2,1)S(1)} %bitcast.14, bf16[2048,576]{0,1:T(8,128)(2,1)S(1)} %copy-done), kind=kOutput, calls=%fused_computation.12 | convolution fusion | flops 905969664 | bytes 5947392 | tf_op jit(solution)/shard_map/dot_general | solution.py:18
  25.7 0.0 copy-start.5
  25.7 0.0 reduce-scatter.4.cloned.1.call-update
  25.7 0.0 all-gather.2.cloned.1.call-start
  25.8 0.9 copy-done.5
  26.7 0.2 reduce_max.24
  26.8 43.8 %reduce-scatter.4.cloned.1.call-done = f32[96,2048]{1,0:T(8,128)} async-done(((f32[384,2048]{1,0:T(8,128)}), f32[96,2048]{1,0:T(8,128)}) %reduce-scatter.4.cloned.1.call-update) | async-done | bytes 786448 | tf_op jit(solution)/shard_map/reduce_scatter | solution.py:17
  70.6 0.0 copy-start.1
  70.6 1.3 reduce_max.23
  72.0 17.8 %all-reduce.2 = (f32[96]{0:T(128)S(1)}, f32[96]{0:T(128)S(1)}) all-reduce(bf16[96]{0:T(256)(128)(2,1)S(1)} %reduce_max.24, f32[96]{0:T(128)S(1)} %reduce_max.23), channel_id=1, replica_groups=mesh['layer'=4,'row'=2,'col'=4] {'row','col'}, use_global_device_ids=true, to_apply=%region_7.0 | all-reduce | flops 192 | bytes 1344 | tf_op jit(solution)/shard_map/pmax | solution.py:26
  89.8 1.5 fusion.2
  91.4 3.0 %all-reduce.4 = (f32[96]{0:T(128)}, f32[96]{0:T(128)}) all-reduce(f32[96]{0:T(128)S(1)} %get-tuple-element.8, f32[96]{0:T(128)S(1)} %get-tuple-element.9), channel_id=1, replica_groups=mesh['layer'=4,'row'=2,'col'=4] {'row'}, use_global_device_ids=true, to_apply=%region_9.0 | all-reduce | flops 192 | bytes 1536 | tf_op jit(solution)/shard_map/psum | solution.py:10
  94.3 6.7 %all-reduce.3 = (f32[96]{0:T(128)S(1)}, f32[96]{0:T(128)S(1)}) all-reduce(f32[96]{0:T(128)} %get-tuple-element.6, f32[96]{0:T(128)} %get-tuple-element.7), channel_id=1, replica_groups=mesh['layer'=4,'row'=2,'col'=4] {'col'}, use_global_device_ids=true, to_apply=%region_10.0 | all-reduce | flops 192 | bytes 1536 | tf_op jit(solution)/shard_map/psum | solution.py:11
  101.1 0.0 copy-done.1
  101.1 1.1 fusion.6
  102.2 0.0 all-gather.2.cloned.1.call-update
  102.2 0.0 copy-start.6
  102.2 30.7 %all-gather.2.cloned.1.call-done = bf16[384,2048]{1,0:T(8,128)(2,1)} async-done(((bf16[96,2048]{1,0:T(8,128)(2,1)}), bf16[384,2048]{1,0:T(8,128)(2,1)}) %all-gather.2.cloned.1.call-update) | async-done | bytes 1572880 | tf_op jit(solution)/shard_map/all_gather | solution.py:35
  132.9 3.8 %fusion.9 = f32[384,576]{1,0:T(8,128)} fusion(bf16[384,2048]{1,0:T(8,128)(2,1)} %all-gather.2.cloned.1.call-done, bf16[2048,576]{0,1:T(8,128)(2,1)S(1)} %copy-done), kind=kOutput, calls=%fused_computation.14 | convolution fusion | flops 905969664 | bytes 4816896 | tf_op jit(solution)/shard_map/dot_general | solution.py:39
  136.7 3.5 %all-to-all-start.1 = ((f32[4,96,576]{2,1,0:T(8,128)}), f32[4,96,576]{2,1,0:T(8,128)S(1)}, u32[]{:S(2)}, u32[]{:S(2)}) async-start(f32[4,96,576]{2,1,0:T(8,128)} %bitcast.17), calls=%async_computation.2 | async-start | bytes 1966080 | tf_op jit(solution)/shard_map/all_to_all | solution.py:40
  140.2 0.0 copy-done.6
  140.2 0.6 dynamic-slice.4
  141.5 11.2 %all-to-all-done.1 = f32[4,96,576]{2,1,0:T(8,128)S(1)} async-done(((f32[4,96,576]{2,1,0:T(8,128)}), f32[4,96,576]{2,1,0:T(8,128)S(1)}, u32[]{:S(2)}, u32[]{:S(2)}) %all-to-all-start.1) | async-done | bytes 884768 | tf_op jit(solution)/shard_map/all_to_all | solution.py:40
  152.6 0.0 copy-start.4
  152.6 0.9 copy-done.4
  153.6 0.0 copy-start.3
  153.6 2.8 %copy.13 = f32[96,4,576]{2,1,0:T(4,128)} copy(f32[96,4,576]{2,0,1:T(8,128)} %bitcast.16) | data formatting | bytes 1769472 | tf_op jit(solution)/shard_map/all_to_all | solution.py:40
  156.4 2.7 %all_to_all.35 = f32[96,2304]{1,0:T(8,128)} reshape(f32[96,4,576]{2,1,0:T(4,128)} %copy.13) | data formatting | bytes 1769472 | tf_op jit(solution)/shard_map/all_to_all | solution.py:40
  159.1 32.7 %fusion = f32[16,2304]{1,0:T(8,128)S(1)} fusion(f32[96,2304]{1,0:T(8,128)} %all_to_all.35), kind=kCustom, calls=%all-reduce-scatter | all-reduce-scatter fusion | flops 294913 | bytes 1032704
  191.8 1.9 collective-permute-start
  193.8 2.4 %collective-permute-start.1 = (f32[12,2304]{1,0:T(8,128)S(1)}, f32[12,2304]{1,0:T(8,128)S(1)}, u32[]{:S(2)}, u32[]{:S(2)}) collective-permute-start(f32[12,2304]{1,0:T(8,128)S(1)} %slice), channel_id=1, source_target_pairs={{0,2},{1,3},{2,4},{3,5},{4,6},{5,7},{8,10},{9,11},{10,12},{11,13},... | collective-permute-start | bytes 331784
  196.2 0.0 copy-done.3
  196.2 5.0 %fusion.8 = f32[2048,576]{0,1:T(8,128)} fusion(bf16[384,2048]{1,0:T(8,128)(2,1)} %all-gather.2.cloned.1.call-done, bf16[384,576]{1,0:T(8,128)(2,1)S(1)} %bitcast.15), kind=kOutput, calls=%fused_computation.13 | convolution fusion | flops 905969664 | bytes 6733824 | tf_op jit(solution)/shard_map/dot_general | solution.py:36
  201.2 2.0 collective-permute-done.1
  203.3 0.0 collective-permute-done
  203.3 0.4 concatenate
  203.7 0.7 constant_dynamic-slice_fusion
  (3 shorter events, 0.0 us)
Async XLA Ops:
  7.2 15.5 %copy-start = (bf16[2048,576]{0,1:T(8,128)(2,1)S(1)}, bf16[2048,576]{0,1:T(8,128)(2,1)}, u32[]{:S(2)}) copy-start(bf16[2048,576]{0,1:T(8,128)(2,1)} %param.4) | copy-start | bytes 7077892
  7.2 63.5 %reduce-scatter.4.cloned.1.call-start = ((), (), s32[]{:S(2)}) async-start(), calls=%async_computation.3 | async-start | bytes 3932160 | tf_op jit(solution)/shard_map/reduce_scatter | solution.py:17
  21.8 0.8 copy-start.2
  25.7 1.0 copy-start.5
  25.7 107.2 %all-gather.2.cloned.1.call-start = ((), (), s32[]{:S(2)}) async-start(), calls=%async_computation.4 | async-start | bytes 1966080 | tf_op jit(solution)/shard_map/all_gather | solution.py:35
  70.6 30.4 %copy-start.1 = (f32[96,2048]{1,0:T(8,128)S(1)}, f32[96,2048]{1,0:T(8,128)}, u32[]{:S(2)}) copy-start(f32[96,2048]{1,0:T(8,128)} %reduce-scatter.4.cloned.1.call-done) | copy-start | bytes 2359300
  102.2 38.0 %copy-start.6 = (u32[32]{0:T(128)S(1)}, u32[32]{0:T(128)}, u32[]{:S(2)}) copy-start(u32[32]{0:T(128)} %constant.10) | copy-start | bytes 388
  136.7 15.9 %all-to-all-start.1 = ((f32[4,96,576]{2,1,0:T(8,128)}), f32[4,96,576]{2,1,0:T(8,128)S(1)}, u32[]{:S(2)}, u32[]{:S(2)}) async-start(f32[4,96,576]{2,1,0:T(8,128)} %bitcast.17), calls=%async_computation.2 | async-start | bytes 1966080 | tf_op jit(solution)/shard_map/all_to_all | solution.py:40
  152.6 0.9 copy-start.4
  153.6 42.6 %copy-start.3 = (bf16[96,4,576]{2,0,1:T(8,128)(2,1)S(1)}, bf16[96,4,576]{2,0,1:T(8,128)(2,1)}, u32[]{:S(2)}) copy-start(bf16[96,4,576]{2,0,1:T(8,128)(2,1)} %copy-done.2) | copy-start | bytes 1327108
  191.8 11.4 %collective-permute-start = (f32[16,2304]{1,0:T(8,128)S(1)}, f32[16,2304]{1,0:T(8,128)S(1)}, u32[]{:S(2)}, u32[]{:S(2)}) collective-permute-start(f32[16,2304]{1,0:T(8,128)S(1)} %fusion), channel_id=1, source_target_pairs={{0,1},{1,2},{2,3},{3,4},{4,5},{5,6},{6,7},{8,9},{9,10},{10,11},{11... | collective-permute-start | bytes 442376
  193.8 9.5 %collective-permute-start.1 = (f32[12,2304]{1,0:T(8,128)S(1)}, f32[12,2304]{1,0:T(8,128)S(1)}, u32[]{:S(2)}, u32[]{:S(2)}) collective-permute-start(f32[12,2304]{1,0:T(8,128)S(1)} %slice), channel_id=1, source_target_pairs={{0,2},{1,3},{2,4},{3,5},{4,6},{5,7},{8,10},{9,11},{10,12},{11,13},... | collective-permute-start | bytes 331784
Sparse Core Ops, SparseCore 0:
  25.8 44.7 reduce-scatter.3
  102.3 30.5 all-gather.1
